TPU v7x, 32 devices: a whole 2x2x4 slice. The times are simulated.
32 devices in a mesh: dp: 16 (over z, y, x), tensor: 2 (over core).
Axes of the slice: x: 2, y: 2, z: 4, core: 2. Of those that a mesh axis runs over, the one named last changes fastest.
Arguments:
- inputs: bfloat16 [4, 8192, 768], P(None, ('dp', 'tensor')), may hold values from -6 to 6
- lengths: int32 [4, 16], P(None, 'dp'), may hold values from 128 to 512, as said below
- bounds: int32 [4, 16], P(None, 'dp'), may hold values from 32 to 384, as said below
- query_matrix: bfloat16 [768, 768], P('dp', 'tensor'), may hold values from -0.21875 to 0.21875
- key_matrix: bfloat16 [768, 768], P('dp', 'tensor'), may hold values from -0.21875 to 0.21875
- value_matrix: bfloat16 [768, 768], P('dp', 'tensor'), may hold values from -0.21875 to 0.21875
- query_value_bias: float32 [2, 768], P(None, 'tensor'), may hold values from -3 to 3
- adapter_down_weight: bfloat16 [2, 768, 8], P(None, 'dp'), may hold values from -0.21875 to 0.21875
- adapter_up_weight: bfloat16 [2, 8, 768], P(None, None, 'tensor'), may hold values from -1 to 1
- attention_output_weight: bfloat16 [768, 768], P('tensor', 'dp'), may hold values from -1.75 to 1.75
- feedforward_input_weight: bfloat16 [768, 3072], P('dp', 'tensor'), may hold values from -0.21875 to 0.21875
- feedforward_input_bias: float32 [3072], P('tensor'), may hold values from -3 to 3
- feedforward_output_weight: bfloat16 [3072, 768], P('tensor', 'dp'), may hold values from -0.109375 to 0.109375
- output_bias: float32 [2, 768], replicated, may hold values from -3 to 3
- layernorm_scale: float32 [2, 768], replicated, may hold values from 0.5 to 1.5
- layernorm_bias: float32 [2, 768], replicated, may hold values from -2 to 2
- output_gradient: bfloat16 [4, 8192, 768], P(None, ('dp', 'tensor')), may hold values from -6 to 6
Outputs:
- outputs: bfloat16 [4, 8192, 768], P(None, ('dp', 'tensor'))
- input_grad: float32 [4, 8192, 768], P(None, ('dp', 'tensor'))
- lora_up_grad: float32 [2, 8, 768], P(None, None, 'tensor')
Inputs may be any that keep to these rules, and one draw needn't show every extreme that they name: Item i of micro-batch m has live positions 0 to lengths[m, i] - 1 of its 512; the others are padding. An item's first segment is positions 0 to bounds - 1, its second bounds to 511; bounds lies between lengths // 4 and 3 * lengths // 4.
All inputs are finite; a program needn't handle non-finite values.
Results may differ from a plain program's by a relative error of at most 0.015.
The roundings to bfloat16 on the way count: a program that leaves them out, or rounds other values in their place, can miss the bound.
Values may be sent and summed in bfloat16 or wider, within the bound.
No kernel may reach another device: no remote copies, remote signals or barrier semaphores. Data moves between devices by JAX's collectives and lax.ppermute only.
A program may use at most 192 MiB of HBM per device.

v0:
```python
import jax
import jax.numpy as jnp
from jax import lax
from jax.sharding import PartitionSpec as P

HEAD_DIM = 64
UPDATE_RANK = 8
SLOT = 512
adapter_scale = 2.0
masked_value = -1000000000.0
norm_eps = 1e-05
highest_precision = lax.Precision.HIGHEST


def layer_norm(value_rows, gain, shift):
    centre = value_rows - jnp.mean(value_rows, axis=-1, keepdims=True)
    spread = jnp.mean(centre * centre, axis=-1, keepdims=True)
    return centre * lax.rsqrt(spread + norm_eps) * gain + shift


def exact_gelu(value_rows):
    return jax.nn.gelu(value_rows, approximate=False)


def item_mask(length, bound):
    places = jnp.arange(SLOT)
    segment = places >= bound
    return (places < length)[None, :] & (segment[:, None] == segment[None, :])


def split_heads(input_array):
    return input_array.reshape(input_array.shape[0], input_array.shape[1] // HEAD_DIM, HEAD_DIM)


def item_scores(query_heads, key_heads, length, bound):
    scores = (
        jnp.einsum("qhd,khd->hqk", query_heads, key_heads, preferred_element_type=jnp.float32)
        * 0.125
    )
    return jnp.where(item_mask(length, bound)[None], scores, masked_value)


def attend_forward(pieces):
    query_rows, keys, value_rows, length, bound = pieces
    query_heads = split_heads(query_rows)
    value_heads = split_heads(value_rows)
    scores = item_scores(query_heads, split_heads(keys), length, bound)
    peak = jnp.max(scores, axis=-1, keepdims=True)
    totals = jnp.log(jnp.sum(jnp.exp(scores - peak), axis=-1, keepdims=True)) + peak
    soft_weights = jnp.exp(scores - totals).astype(jnp.bfloat16)
    mixed = jnp.einsum(
        "hqk,khd->qhd", soft_weights, value_heads, preferred_element_type=jnp.float32
    )
    return (mixed.reshape(SLOT, query_rows.shape[1]).astype(jnp.bfloat16), totals)


def attend_backward(pieces):
    query_rows, keys, value_rows, grad_mixed, totals, length, bound = pieces
    query_heads = split_heads(query_rows)
    key_heads = split_heads(keys)
    grad_heads = split_heads(grad_mixed)
    scores = item_scores(query_heads, key_heads, length, bound)
    probs = jnp.exp(scores - totals)
    value_gradient = jnp.einsum(
        "hqk,qhd->khd", probs.astype(jnp.bfloat16), grad_heads, preferred_element_type=jnp.float32
    )
    grad_probs = jnp.einsum(
        "qhd,khd->hqk", grad_heads, split_heads(value_rows), preferred_element_type=jnp.float32
    )
    inner = jnp.sum(probs * grad_probs, axis=-1, keepdims=True)
    grad_scores = (probs * (grad_probs - inner)).astype(jnp.bfloat16)
    query_gradient = (
        jnp.einsum("hqk,khd->qhd", grad_scores, key_heads, preferred_element_type=jnp.float32)
        * 0.125
    )
    key_gradient = (
        jnp.einsum("hqk,qhd->khd", grad_scores, query_heads, preferred_element_type=jnp.float32)
        * 0.125
    )
    width = query_rows.shape[1]
    return (
        query_gradient.reshape(SLOT, width).astype(jnp.bfloat16),
        key_gradient.reshape(SLOT, width).astype(jnp.bfloat16),
        value_gradient.reshape(SLOT, width).astype(jnp.bfloat16),
    )


def contract_trailing(left, right):
    return lax.dot_general(
        left, right, (((1,), (1,)), ((), ())), preferred_element_type=jnp.float32
    )


def project_row_batch(
    input_rows,
    query_projected,
    key_projected,
    value_projected,
    down_projected,
    query_value_bias,
    adapter_up_weight,
):
    up_weight_float = adapter_up_weight.astype(jnp.float32)
    lowrank_update = jnp.einsum(
        "td,zdr->ztr", input_rows, down_projected, preferred_element_type=jnp.float32
    )
    query_rows = (
        jnp.dot(input_rows, query_projected, preferred_element_type=jnp.float32)
        + query_value_bias[0]
        + adapter_scale
        * jnp.dot(lowrank_update[0], up_weight_float[0], precision=highest_precision)
    ).astype(jnp.bfloat16)
    keys = jnp.dot(input_rows, key_projected, preferred_element_type=jnp.float32).astype(
        jnp.bfloat16
    )
    value_rows = (
        jnp.dot(input_rows, value_projected, preferred_element_type=jnp.float32)
        + query_value_bias[1]
        + adapter_scale
        * jnp.dot(lowrank_update[1], up_weight_float[1], precision=highest_precision)
    ).astype(jnp.bfloat16)
    return (lowrank_update, query_rows, keys, value_rows)


def adapter_components(lowrank_update, query_gradient, value_gradient):
    first_dims = (((0,), (0,)), ((), ()))
    return adapter_scale * jnp.stack(
        [
            lax.dot_general(
                lowrank_update[0],
                query_gradient.astype(jnp.float32),
                first_dims,
                precision=highest_precision,
            ),
            lax.dot_general(
                lowrank_update[1],
                value_gradient.astype(jnp.float32),
                first_dims,
                precision=highest_precision,
            ),
        ]
    )


def input_terms_all(
    query_gradient,
    key_gradient,
    value_gradient,
    query_projected,
    key_projected,
    value_projected,
    down_projected,
    adapter_up_weight,
):
    query_lowrank_gradient = adapter_scale * contract_trailing(query_gradient, adapter_up_weight[0])
    value_lowrank_gradient = adapter_scale * contract_trailing(value_gradient, adapter_up_weight[1])
    down_float = down_projected.astype(jnp.float32)
    total = contract_trailing(query_gradient, query_projected)
    total = total + contract_trailing(key_gradient, key_projected)
    total = total + contract_trailing(value_gradient, value_projected)
    total = total + lax.dot_general(
        query_lowrank_gradient, down_float[0], (((1,), (1,)), ((), ())), precision=highest_precision
    )
    total = total + lax.dot_general(
        value_lowrank_gradient, down_float[1], (((1,), (1,)), ((), ())), precision=highest_precision
    )
    return total


def forward_pass(rows_local, item_lengths, item_bounds, gathered, parameters):
    (
        query_projected,
        key_projected,
        value_projected,
        down_projected,
        out_full,
        ffn_in_full,
        ffn_out_full,
    ) = gathered
    (
        query_value_bias,
        adapter_up_weight,
        feedforward_input_bias,
        output_bias,
        layernorm_scale,
        layernorm_bias,
    ) = parameters
    group_items = item_lengths.shape[0]
    row_groups = lax.all_gather(rows_local, "tensor", axis=0, tiled=True)
    lowrank_update, query_rows, keys, value_rows = project_row_batch(
        row_groups,
        query_projected,
        key_projected,
        value_projected,
        down_projected,
        query_value_bias,
        adapter_up_weight,
    )
    width = query_rows.shape[1]
    item_shape = (group_items, SLOT, width)
    mixed, totals = lax.map(
        attend_forward,
        (
            query_rows.reshape(item_shape),
            keys.reshape(item_shape),
            value_rows.reshape(item_shape),
            item_lengths,
            item_bounds,
        ),
    )
    mixed_rows = mixed.reshape(group_items * SLOT, width)
    attended = lax.psum_scatter(
        jnp.dot(mixed_rows, out_full, preferred_element_type=jnp.float32),
        "tensor",
        scatter_dimension=0,
        tiled=True,
    )
    hidden_sum = rows_local.astype(jnp.float32) + attended + output_bias[0]
    normed = layer_norm(hidden_sum, layernorm_scale[0], layernorm_bias[0])
    pre_act = (
        jnp.dot(
            lax.all_gather(normed.astype(jnp.bfloat16), "tensor", axis=0, tiled=True),
            ffn_in_full,
            preferred_element_type=jnp.float32,
        )
        + feedforward_input_bias
    )
    activated = exact_gelu(pre_act).astype(jnp.bfloat16)
    ffn_total = (
        normed
        + lax.psum_scatter(
            jnp.dot(activated, ffn_out_full, preferred_element_type=jnp.float32),
            "tensor",
            scatter_dimension=0,
            tiled=True,
        )
        + output_bias[1]
    )
    result = layer_norm(ffn_total, layernorm_scale[1], layernorm_bias[1]).astype(jnp.bfloat16)
    kept = (lowrank_update, query_rows, keys, value_rows, totals, hidden_sum, pre_act, ffn_total)
    return (result, kept)


def layer_backward(grad_out, item_lengths, item_bounds, gathered, parameters, kept):
    (
        query_projected,
        key_projected,
        value_projected,
        down_projected,
        out_full,
        ffn_in_full,
        ffn_out_full,
    ) = gathered
    (
        query_value_bias,
        adapter_up_weight,
        feedforward_input_bias,
        output_bias,
        layernorm_scale,
        layernorm_bias,
    ) = parameters
    lowrank_update, query_rows, keys, value_rows, totals, hidden_sum, pre_act, ffn_total = kept
    group_items = item_lengths.shape[0]
    outer_pull = jax.vjp(
        lambda field: layer_norm(field, layernorm_scale[1], layernorm_bias[1]), ffn_total
    )[1]
    grad_sum = outer_pull(grad_out.astype(jnp.float32))[0]
    grad_act = contract_trailing(
        lax.all_gather(grad_sum.astype(jnp.bfloat16), "tensor", axis=0, tiled=True), ffn_out_full
    )
    gelu_pull = jax.vjp(exact_gelu, pre_act)[1]
    grad_pre = gelu_pull(grad_act)[0].astype(jnp.bfloat16)
    grad_normed = grad_sum + lax.psum_scatter(
        contract_trailing(grad_pre, ffn_in_full), "tensor", scatter_dimension=0, tiled=True
    )
    inner_pull = jax.vjp(
        lambda field: layer_norm(field, layernorm_scale[0], layernorm_bias[0]), hidden_sum
    )[1]
    grad_hidden = inner_pull(grad_normed)[0]
    grad_mixed = contract_trailing(
        lax.all_gather(grad_hidden.astype(jnp.bfloat16), "tensor", axis=0, tiled=True), out_full
    ).astype(jnp.bfloat16)
    width = query_rows.shape[1]
    item_shape = (group_items, SLOT, width)
    query_gradient, key_gradient, value_gradient = lax.map(
        attend_backward,
        (
            query_rows.reshape(item_shape),
            keys.reshape(item_shape),
            value_rows.reshape(item_shape),
            grad_mixed.reshape(item_shape),
            totals,
            item_lengths,
            item_bounds,
        ),
    )
    query_gradient = query_gradient.reshape(group_items * SLOT, width)
    key_gradient = key_gradient.reshape(group_items * SLOT, width)
    value_gradient = value_gradient.reshape(group_items * SLOT, width)
    adapter_portion = adapter_components(lowrank_update, query_gradient, value_gradient)
    row_gradient = grad_hidden + lax.psum_scatter(
        input_terms_all(
            query_gradient,
            key_gradient,
            value_gradient,
            query_projected,
            key_projected,
            value_projected,
            down_projected,
            adapter_up_weight,
        ).astype(jnp.bfloat16),
        "tensor",
        scatter_dimension=0,
        tiled=True,
    ).astype(jnp.float32)
    return (row_gradient, adapter_portion)


def local(
    inputs,
    lengths,
    bounds,
    query_matrix,
    key_matrix,
    value_matrix,
    query_value_bias,
    adapter_down_weight,
    adapter_up_weight,
    attention_output_weight,
    feedforward_input_weight,
    feedforward_input_bias,
    feedforward_output_weight,
    output_bias,
    layernorm_scale,
    layernorm_bias,
    output_gradient,
):
    micro_count = inputs.shape[0]
    parameters = (
        query_value_bias,
        adapter_up_weight,
        feedforward_input_bias,
        output_bias,
        layernorm_scale,
        layernorm_bias,
    )
    result_list = []
    gradient_tree = []
    adapter_combined = jnp.zeros((2, UPDATE_RANK, adapter_up_weight.shape[2]), jnp.float32)
    for batch_index in range(micro_count):
        forward_set = (
            lax.all_gather(query_matrix, "dp", axis=0, tiled=True),
            lax.all_gather(key_matrix, "dp", axis=0, tiled=True),
            lax.all_gather(value_matrix, "dp", axis=0, tiled=True),
            lax.all_gather(adapter_down_weight, "dp", axis=1, tiled=True),
            lax.all_gather(attention_output_weight, "dp", axis=1, tiled=True),
            lax.all_gather(feedforward_input_weight, "dp", axis=0, tiled=True),
            lax.all_gather(feedforward_output_weight, "dp", axis=1, tiled=True),
        )
        result, kept = forward_pass(
            inputs[batch_index], lengths[batch_index], bounds[batch_index], forward_set, parameters
        )
        backward_set = (
            lax.all_gather(query_matrix, "dp", axis=0, tiled=True),
            lax.all_gather(key_matrix, "dp", axis=0, tiled=True),
            lax.all_gather(value_matrix, "dp", axis=0, tiled=True),
            lax.all_gather(adapter_down_weight, "dp", axis=1, tiled=True),
            lax.all_gather(attention_output_weight, "dp", axis=1, tiled=True),
            lax.all_gather(feedforward_input_weight, "dp", axis=0, tiled=True),
            lax.all_gather(feedforward_output_weight, "dp", axis=1, tiled=True),
        )
        row_gradient, adapter_portion = layer_backward(
            output_gradient[batch_index],
            lengths[batch_index],
            bounds[batch_index],
            backward_set,
            parameters,
            kept,
        )
        adapter_combined = adapter_combined + lax.psum(adapter_portion, "dp")
        result_list.append(result)
        gradient_tree.append(row_gradient)
    return (jnp.stack(result_list), jnp.stack(gradient_tree), adapter_combined)


def solution(mesh):
    return jax.shard_map(
        local,
        mesh=mesh,
        in_specs=(
            P(None, ("dp", "tensor"), None),
            P(None, "dp"),
            P(None, "dp"),
            P("dp", "tensor"),
            P("dp", "tensor"),
            P("dp", "tensor"),
            P(None, "tensor"),
            P(None, "dp", None),
            P(None, None, "tensor"),
            P("tensor", "dp"),
            P("dp", "tensor"),
            P("tensor"),
            P("tensor", "dp"),
            P(),
            P(),
            P(),
            P(None, ("dp", "tensor"), None),
        ),
        out_specs=(
            P(None, ("dp", "tensor"), None),
            P(None, ("dp", "tensor"), None),
            P(None, None, "tensor"),
        ),
        check_vma=False,
    )
```

profile of v0, /device:TPU:0, one launch (start us, length us, event | category | flops | bytes accessed | tf_op | source)
XLA Modules:
  0.0 771.6 jit_solution(13941130316083166364)
XLA Ops:
  12.5 44.5 %all_gather.48 = bf16[2,768,8]{2,0,1:T(2,128)(2,1)S(1)} all-gather(bf16[2,48,8]{2,0,1:T(2,128)(2,1)S(1)} %copy.57), channel_id=1, replica_groups=mesh['dp'=16,'tensor'=2] {'dp'}, dimensions={1}, use_global_device_ids=true | all-gather | bytes 26112 | tf_op jit(solution)/shard_map/all_gather | solution.py:355
  57.3 39.2 %all_gather.49 = bf16[768,384]{1,0:T(8,128)(2,1)S(1)} all-gather(bf16[48,384]{1,0:T(8,128)(2,1)} %param.20), channel_id=1, replica_groups=mesh['dp'=16,'tensor'=2] {'dp'}, dimensions={0}, use_global_device_ids=true | all-gather | bytes 626688 | tf_op jit(solution)/shard_map/all_gather | solution.py:352
  96.5 41.1 %all_gather.50 = bf16[768,384]{1,0:T(8,128)(2,1)S(1)} all-gather(bf16[48,384]{1,0:T(8,128)(2,1)} %param.21), channel_id=1, replica_groups=mesh['dp'=16,'tensor'=2] {'dp'}, dimensions={0}, use_global_device_ids=true | all-gather | bytes 626688 | tf_op jit(solution)/shard_map/all_gather | solution.py:353
  137.5 39.3 %all_gather.47 = bf16[768,384]{1,0:T(8,128)(2,1)S(1)} all-gather(bf16[48,384]{1,0:T(8,128)(2,1)} %param.22), channel_id=1, replica_groups=mesh['dp'=16,'tensor'=2] {'dp'}, dimensions={0}, use_global_device_ids=true | all-gather | bytes 626688 | tf_op jit(solution)/shard_map/all_gather | solution.py:354
  176.8 40.8 %all_gather.51 = bf16[384,768]{0,1:T(8,128)(2,1)S(1)} all-gather(bf16[384,48]{0,1:T(8,128)(2,1)} %param.26), channel_id=1, replica_groups=mesh['dp'=16,'tensor'=2] {'dp'}, dimensions={1}, use_global_device_ids=true | all-gather | bytes 626688 | tf_op jit(solution)/shard_map/all_gather | solution.py:356
  232.9 3.3 all-gather
  247.4 3.1 all-gather.3
  261.4 3.2 all-gather.2
  278.0 2.6 reduce-scatter.25.cloned.1.call-done
  280.6 4.3 fusion.188
  286.7 2.8 all_gather.60
  289.5 47.2 %all-gather.7.cloned.1.call-done = bf16[768,1536]{1,0:T(8,128)(2,1)} async-done(((bf16[48,1536]{1,0:T(8,128)(2,1)}), bf16[768,1536]{1,0:T(8,128)(2,1)}) %all-gather.7.cloned.1.call-update) | async-done | bytes 2359312 | tf_op jit(solution)/shard_map/all_gather | solution.py:357
  336.7 10.4 %fusion.11 = (f32[512,1536]{1,0:T(8,128)}, f32[512,1536]{1,0:T(8,128)}) fusion(f32[1536]{0:T(1024)S(1)} %copy-done.198, bf16[512,768]{1,0:T(8,128)(2,1)S(1)} %all_gather.60, bf16[768,1536]{1,0:T(8,128)(2,1)} %all-gather.7.cloned.1.call-done), kind=kOutput, calls=%fused_computation.39 | convolution fusion | flops 1257504768 | bytes 9443328 | tf_op jit(solution)/shard_map/dot_general | solution.py:221
  347.2 52.7 %all-gather.9.cloned.1.call-done = bf16[1536,768]{0,1:T(8,128)(2,1)} async-done(((bf16[1536,48]{0,1:T(8,128)(2,1)}), bf16[1536,768]{0,1:T(8,128)(2,1)}) %all-gather.9.cloned.1.call-update) | async-done | bytes 2359312 | tf_op jit(solution)/shard_map/all_gather | solution.py:358
  399.9 6.1 fusion.35
  408.4 9.7 %fusion.10 = (f32[512,1536]{1,0:T(8,128)S(1)}, f32[512,1536]{1,0:T(8,128)S(1)}) fusion(f32[1536]{0:T(1024)} %param.28, bf16[512,768]{1,0:T(8,128)(2,1)S(1)} %all_gather.58, bf16[768,1536]{1,0:T(8,128)(2,1)} %all-gather.7.cloned.1.call-done), kind=kOutput, calls=%fused_computation.38 | convolution fusion | flops 1257504768 | bytes 9443328 | tf_op jit(solution)/shard_map/dot_general | solution.py:221
  420.8 2.7 fusion.34
  425.9 9.5 %fusion.9 = (f32[512,1536]{1,0:T(8,128)S(1)}, f32[512,1536]{1,0:T(8,128)S(1)}) fusion(f32[1536]{0:T(1024)} %param.28, bf16[512,768]{1,0:T(8,128)(2,1)S(1)} %all_gather.56, bf16[768,1536]{1,0:T(8,128)(2,1)} %all-gather.7.cloned.1.call-done), kind=kOutput, calls=%fused_computation.37 | convolution fusion | flops 1257504768 | bytes 9443328 | tf_op jit(solution)/shard_map/dot_general | solution.py:221
  438.1 2.6 fusion.33
  442.4 5.9 reduce-scatter.23.cloned.1.call-done
  448.4 4.5 fusion.187
  455.2 8.1 %fusion.8 = (f32[512,1536]{1,0:T(8,128)S(1)}, f32[512,1536]{1,0:T(8,128)S(1)}) fusion(f32[1536]{0:T(1024)S(1)} %copy-done.199, bf16[512,768]{1,0:T(8,128)(2,1)S(1)} %all_gather.52, bf16[768,1536]{1,0:T(8,128)(2,1)S(1)} %copy-done.197), kind=kOutput, calls=%fused_computation.36 | convolution fusion | flops 1257504768 | bytes 9443328 | tf_op jit(solution)/shard_map/dot_general | solution.py:221
  466.0 2.6 fusion.32
  468.7 10.4 %reduce-scatter.19.cloned.1.call-done = f32[256,768]{1,0:T(8,128)} async-done(((f32[512,768]{1,0:T(8,128)}), f32[256,768]{1,0:T(8,128)}) %reduce-scatter.19.cloned.1.call-update) | async-done | bytes 786448 | tf_op jit(solution)/shard_map/reduce_scatter | solution.py:231
  481.0 3.5 fusion.79
  486.7 2.5 all_gather.67
  489.2 7.8 %fusion.43 = f32[512,768]{1,0:T(8,128)} fusion(bf16[768,1536]{1,0:T(8,128)(2,1)} %all-gather.7.cloned.1.call-done, f32[512,1536]{1,0:T(8,128)} %get-tuple-element.339, f32[512,1536]{1,0:T(8,128)} %get-tuple-element.340, bf16[512,768]{1,0:T(8,128)(2,1)} %all_gather.67, bf16[1536,768]{0,1:T(8,128)(2,1)S(1)} %copy-done.4), kind=kOutput, calls=%fused_computation.117 | convolution fusion | flops 2426929152 | bytes 13369344 | tf_op jit(solution)/shard_map/dot_general | solution.py:89
  499.1 4.4 fusion.181
  507.1 7.8 %fusion.42 = f32[512,768]{1,0:T(8,128)} fusion(bf16[768,1536]{1,0:T(8,128)(2,1)} %all-gather.7.cloned.1.call-done, f32[512,1536]{1,0:T(8,128)} %copy-done.82, f32[512,1536]{1,0:T(8,128)} %copy-done.83, bf16[512,768]{1,0:T(8,128)(2,1)} %all_gather.65, bf16[1536,768]{0,1:T(8,128)(2,1)S(1)} %copy-done.4), kind=kOutput, calls=%fused_computation.116 | convolution fusion | flops 2426929152 | bytes 13369344 | tf_op jit(solution)/shard_map/dot_general | solution.py:89
  516.2 2.9 all_gather.61
  519.1 8.3 %fusion.40 = f32[512,768]{1,0:T(8,128)} fusion(bf16[768,1536]{1,0:T(8,128)(2,1)} %all-gather.7.cloned.1.call-done, f32[512,1536]{1,0:T(8,128)} %copy-done.84, f32[512,1536]{1,0:T(8,128)} %copy-done.85, bf16[512,768]{1,0:T(8,128)(2,1)} %all_gather.61, bf16[1536,768]{0,1:T(8,128)(2,1)S(1)} %copy-done.4), kind=kOutput, calls=%fused_computation.114 | convolution fusion | flops 2426929152 | bytes 13369344 | tf_op jit(solution)/shard_map/dot_general | solution.py:89
  531.3 7.8 %fusion.41 = f32[512,768]{1,0:T(8,128)} fusion(bf16[768,1536]{1,0:T(8,128)(2,1)} %all-gather.7.cloned.1.call-done, f32[512,1536]{1,0:T(8,128)} %copy-done.80, f32[512,1536]{1,0:T(8,128)} %copy-done.81, bf16[512,768]{1,0:T(8,128)(2,1)} %all_gather.63, bf16[1536,768]{0,1:T(8,128)(2,1)S(1)} %copy-done.4), kind=kOutput, calls=%fused_computation.115 | convolution fusion | flops 2426929152 | bytes 13369344 | tf_op jit(solution)/shard_map/dot_general | solution.py:89
  539.2 2.7 pad_maximum_fusion.1
  542.1 3.1 multiply_reduce_fusion.7
  545.2 5.8 reduce-scatter.37.cloned.1.call-done
  551.0 2.5 fusion.179
  556.9 4.6 convolution_convert_fusion.6
  580.7 2.5 all_gather.68
  588.9 4.6 multiply_reduce_fusion.3
  593.6 6.5 multiply_convert_fusion.3
  603.3 4.8 multiply_reduce_fusion.2
  608.2 4.7 multiply_reduce_fusion.1
  612.8 5.6 multiply_reduce_fusion
  622.1 6.7 multiply_convert_fusion.2
  630.5 4.9 multiply_convert_fusion.1
  637.3 4.7 multiply_convert_fusion
  676.5 77.1 %psum.34 = f32[2,8,384]{2,1,0:T(8,128)} all-reduce(f32[2,8,384]{2,1,0:T(8,128)S(1)} %fusion.110), channel_id=1, replica_groups=mesh['dp'=16,'tensor'=2] {'dp'}, use_global_device_ids=true, to_apply=%region_60.61 | all-reduce | flops 6144 | bytes 49152 | tf_op jit(solution)/shard_map/psum | solution.py:380
  761.0 3.1 pad_maximum_fusion
  (654 shorter events, 167.3 us)
Async XLA Ops:
  8.0 270.0 %reduce-scatter.21.cloned.1.call-start = ((), (), s32[]{:S(2)}) async-start(), calls=%async_computation.20 | async-start | bytes 2359296 | tf_op jit(solution)/shard_map/reduce_scatter | solution.py:212
  57.3 207.3 %copy-start.88 = (bf16[2,768,8]{1,2,0:T(8,128)(2,1)}, bf16[2,768,8]{1,2,0:T(8,128)(2,1)S(1)}, u32[]{:S(2)}) copy-start(bf16[2,768,8]{1,2,0:T(8,128)(2,1)S(1)} %copy.58) | copy-start | bytes 73732
  57.3 160.3 %copy-start.53 = (bf16[4,256,768]{2,1,0:T(8,128)(2,1)S(1)}, bf16[4,256,768]{2,1,0:T(8,128)(2,1)}, u32[]{:S(2)}) copy-start(bf16[4,256,768]{2,1,0:T(8,128)(2,1)} %param.17) | copy-start | bytes 4718596
  96.5 168.4 %copy-start.19 = (bf16[768,384]{1,0:T(8,128)(2,1)}, bf16[768,384]{1,0:T(8,128)(2,1)S(1)}, u32[]{:S(2)}) copy-start(bf16[768,384]{1,0:T(8,128)(2,1)S(1)} %all_gather.49) | copy-start | bytes 1769476
  137.5 129.9 %copy-start.14 = (bf16[768,384]{1,0:T(8,128)(2,1)}, bf16[768,384]{1,0:T(8,128)(2,1)S(1)}, u32[]{:S(2)}) copy-start(bf16[768,384]{1,0:T(8,128)(2,1)S(1)} %all_gather.50) | copy-start | bytes 1769476
  176.8 93.8 %copy-start.22 = (bf16[768,384]{1,0:T(8,128)(2,1)}, bf16[768,384]{1,0:T(8,128)(2,1)S(1)}, u32[]{:S(2)}) copy-start(bf16[768,384]{1,0:T(8,128)(2,1)S(1)} %all_gather.47) | copy-start | bytes 1769476
  217.6 56.1 %copy-start.24 = (bf16[384,768]{0,1:T(8,128)(2,1)}, bf16[384,768]{0,1:T(8,128)(2,1)S(1)}, u32[]{:S(2)}) copy-start(bf16[384,768]{0,1:T(8,128)(2,1)S(1)} %all_gather.51) | copy-start | bytes 1769476
  232.9 45.1 %reduce-scatter.17.cloned.1.call-start = ((), (), s32[]{:S(2)}) async-start(), calls=%async_computation.16 | async-start | bytes 2359296 | tf_op jit(solution)/shard_map/reduce_scatter | solution.py:212
  247.3 30.7 %reduce-scatter.29.cloned.1.call-start = ((), (), s32[]{:S(2)}) async-start(), calls=%async_computation.24 | async-start | bytes 2359296 | tf_op jit(solution)/shard_map/reduce_scatter | solution.py:212
  261.3 19.3 %reduce-scatter.25.cloned.1.call-start = ((), (), s32[]{:S(2)}) async-start(), calls=%async_computation.22 | async-start | bytes 2359296 | tf_op jit(solution)/shard_map/reduce_scatter | solution.py:212
  275.5 61.2 %all-gather.7.cloned.1.call-start = ((), (), s32[]{:S(2)}) async-start(), calls=%async_computation.17 | async-start | bytes 2506752 | tf_op jit(solution)/shard_map/all_gather | solution.py:357
  276.1 123.8 %all-gather.9.cloned.1.call-start = ((), (), s32[]{:S(2)}) async-start(), calls=%async_computation.18 | async-start | bytes 2506752 | tf_op jit(solution)/shard_map/all_gather | solution.py:358
  276.7 165.7 %reduce-scatter.31.cloned.1.call-start = ((), (), s32[]{:S(2)}) async-start(), calls=%async_computation.25 | async-start | bytes 2359296 | tf_op jit(solution)/shard_map/reduce_scatter | solution.py:231
  285.1 51.6 %copy-start.198 = (f32[1536]{0:T(1024)S(1)}, f32[1536]{0:T(1024)}, u32[]{:S(2)}) copy-start(f32[1536]{0:T(1024)} %param.28) | copy-start | bytes 18436
  406.0 36.4 %reduce-scatter.27.cloned.1.call-start = ((), (), s32[]{:S(2)}) async-start(), calls=%async_computation.23 | async-start | bytes 2359296 | tf_op jit(solution)/shard_map/reduce_scatter | solution.py:231
  408.4 12.3 %copy-start.4 = (bf16[1536,768]{0,1:T(8,128)(2,1)S(1)}, bf16[1536,768]{0,1:T(8,128)(2,1)}, u32[]{:S(2)}) copy-start(bf16[1536,768]{0,1:T(8,128)(2,1)} %all-gather.9.cloned.1.call-done) | copy-start | bytes 7077892
  423.4 24.9 %reduce-scatter.23.cloned.1.call-start = ((), (), s32[]{:S(2)}) async-start(), calls=%async_computation.21 | async-start | bytes 2359296 | tf_op jit(solution)/shard_map/reduce_scatter | solution.py:231
  438.1 10.2 %copy-start.142 = (f32[768]{0:T(1024)S(1)}, f32[768]{0:T(1024)}, u32[]{:S(2)}) copy-start(f32[768]{0:T(1024)} %get-tuple-element.175) | copy-start | bytes 9220
  438.1 10.2 %copy-start.144 = (f32[256]{0:T(256)S(1)}, f32[256]{0:T(256)}, u32[]{:S(2)}) copy-start(f32[256]{0:T(256)} %copy-done.143) | copy-start | bytes 3076
  438.1 10.2 %copy-start.148 = (f32[256]{0:T(256)S(1)}, f32[256]{0:T(256)}, u32[]{:S(2)}) copy-start(f32[256]{0:T(256)} %copy-done.147) | copy-start | bytes 3076
  438.1 10.2 %copy-start.152 = (f32[256]{0:T(256)S(1)}, f32[256]{0:T(256)}, u32[]{:S(2)}) copy-start(f32[256]{0:T(256)} %copy-done.151) | copy-start | bytes 3076
  438.1 10.2 %copy-start.165 = (f32[256]{0:T(256)S(1)}, f32[256]{0:T(256)}, u32[]{:S(2)}) copy-start(f32[256]{0:T(256)} %copy-done.164) | copy-start | bytes 3076
  438.1 10.2 %copy-start.168 = (f32[256]{0:T(256)S(1)}, f32[256]{0:T(256)}, u32[]{:S(2)}) copy-start(f32[256]{0:T(256)} %copy-done.167) | copy-start | bytes 3076
  438.1 10.2 %copy-start.171 = (f32[256]{0:T(256)S(1)}, f32[256]{0:T(256)}, u32[]{:S(2)}) copy-start(f32[256]{0:T(256)} %copy-done.170) | copy-start | bytes 3076
  440.7 38.3 %reduce-scatter.19.cloned.1.call-start = ((), (), s32[]{:S(2)}) async-start(), calls=%async_computation.19 | async-start | bytes 2359296 | tf_op jit(solution)/shard_map/reduce_scatter | solution.py:231
  442.3 10.6 %copy-start.189 = (f32[256]{0:T(256)}, f32[256]{0:T(256)S(1)}, u32[]{:S(2)}) copy-start(f32[256]{0:T(256)S(1)} %multiply_reduce_fusion.15) | copy-start | bytes 3076
  442.4 36.7 %copy-start.154 = (f32[256]{0:T(256)}, f32[256]{0:T(256)S(1)}, u32[]{:S(2)}) copy-start(f32[256]{0:T(256)S(1)} %fusion.147) | copy-start | bytes 3076
  468.6 73.4 %reduce-scatter.45.cloned.1.call-start = ((), (), s32[]{:S(2)}) async-start(), calls=%async_computation.32 | async-start | bytes 2359296 | tf_op jit(solution)/shard_map/reduce_scatter | solution.py:273
  468.6 15.8 %copy-start.179 = (f32[256]{0:T(256)}, f32[256]{0:T(256)S(1)}, u32[]{:S(2)}) copy-start(f32[256]{0:T(256)S(1)} %broadcast_multiply_fusion.4) | copy-start | bytes 3076
  468.6 15.8 %copy-start.180 = (f32[256]{0:T(256)}, f32[256]{0:T(256)S(1)}, u32[]{:S(2)}) copy-start(f32[256]{0:T(256)S(1)} %broadcast_multiply_fusion.2) | copy-start | bytes 3076
  468.7 15.8 %copy-start.182 = (f32[256]{0:T(256)}, f32[256]{0:T(256)S(1)}, u32[]{:S(2)}) copy-start(f32[256]{0:T(256)S(1)} %broadcast_multiply_fusion) | copy-start | bytes 3076
  489.2 10.0 %copy-start.141 = (f32[768]{0:T(1024)S(1)}, f32[768]{0:T(1024)}, u32[]{:S(2)}) copy-start(f32[768]{0:T(1024)} %get-tuple-element.173) | copy-start | bytes 9220
  497.0 45.0 %reduce-scatter.41.cloned.1.call-start = ((), (), s32[]{:S(2)}) async-start(), calls=%async_computation.30 | async-start | bytes 2359296 | tf_op jit(solution)/shard_map/reduce_scatter | solution.py:273
  503.5 11.4 %copy-start.158 = (f32[256]{0:T(256)}, f32[256]{0:T(256)S(1)}, u32[]{:S(2)}) copy-start(f32[256]{0:T(256)S(1)} %negate_multiply_fusion.7) | copy-start | bytes 3076
  514.9 27.1 %reduce-scatter.33.cloned.1.call-start = ((), (), s32[]{:S(2)}) async-start(), calls=%async_computation.26 | async-start | bytes 2359296 | tf_op jit(solution)/shard_map/reduce_scatter | solution.py:273
  515.0 12.5 %copy-start.162 = (f32[256]{0:T(256)}, f32[256]{0:T(256)S(1)}, u32[]{:S(2)}) copy-start(f32[256]{0:T(256)S(1)} %negate_multiply_fusion.11) | copy-start | bytes 3076
  527.5 23.6 %reduce-scatter.37.cloned.1.call-start = ((), (), s32[]{:S(2)}) async-start(), calls=%async_computation.28 | async-start | bytes 2359296 | tf_op jit(solution)/shard_map/reduce_scatter | solution.py:273
  539.1 214.4 %reduce-scatter.35.cloned.1.call-start = ((), (), s32[]{:S(2)}) async-start(), calls=%async_computation.27 | async-start | bytes 1179648 | tf_op jit(solution)/shard_map/reduce_scatter | solution.py:301
  556.9 10.7 %slice-start = ((s8[6291456]{0:T(1024)(128)(4,1)}), s8[4194304]{0:T(1024)(128)(4,1)S(1)}, s32[]{:S(2)}) async-start(s8[6291456]{0:T(1024)(128)(4,1)} %bitcast.410), calls=%async_computation.34 | async-start | bytes 8388608
  622.1 133.6 %reduce-scatter.39.cloned.1.call-start = ((), (), s32[]{:S(2)}) async-start(), calls=%async_computation.29 | async-start | bytes 1179648 | tf_op jit(solution)/shard_map/reduce_scatter | solution.py:301
  649.9 107.8 %reduce-scatter.43.cloned.1.call-start = ((), (), s32[]{:S(2)}) async-start(), calls=%async_computation.31 | async-start | bytes 1179648 | tf_op jit(solution)/shard_map/reduce_scatter | solution.py:301
  659.8 100.1 %reduce-scatter.47.cloned.1.call-start = ((), (), s32[]{:S(2)}) async-start(), calls=%async_computation.33 | async-start | bytes 1179648 | tf_op jit(solution)/shard_map/reduce_scatter | solution.py:301
  667.1 86.5 %copy-start.174 = (f32[256]{0:T(256)S(1)}, f32[256]{0:T(256)}, u32[]{:S(2)}) copy-start(f32[256]{0:T(256)} %copy-done.173) | copy-start | bytes 3076
  669.2 84.4 %copy-start.33 = (f32[256,768]{1,0:T(8,128)S(1)}, f32[256,768]{1,0:T(8,128)}, u32[]{:S(2)}) copy-start(f32[256,768]{1,0:T(8,128)} %copy-done.32) | copy-start | bytes 2359300
  669.2 86.4 %copy-start.37 = (f32[256,768]{1,0:T(8,128)S(1)}, f32[256,768]{1,0:T(8,128)}, u32[]{:S(2)}) copy-start(f32[256,768]{1,0:T(8,128)} %copy-done.36) | copy-start | bytes 2359300
  669.2 88.5 %copy-start.35 = (f32[256,768]{1,0:T(8,128)S(1)}, f32[256,768]{1,0:T(8,128)}, u32[]{:S(2)}) copy-start(f32[256,768]{1,0:T(8,128)} %copy-done.34) | copy-start | bytes 2359300
  674.2 85.6 %copy-start.40 = (f32[256,768]{1,0:T(8,128)S(1)}, f32[256,768]{1,0:T(8,128)}, u32[]{:S(2)}) copy-start(f32[256,768]{1,0:T(8,128)} %copy-done.39) | copy-start | bytes 2359300
  674.2 85.6 %copy-start.178 = (f32[256]{0:T(256)S(1)}, f32[256]{0:T(256)}, u32[]{:S(2)}) copy-start(f32[256]{0:T(256)} %copy-done.177) | copy-start | bytes 3076
  (184 other events, 702.5 us)
Sparse Core Ops, SparseCore 0:
  233.0 5.0 reduce-scatter.20
  247.4 5.1 reduce-scatter.16
  261.5 5.1 reduce-scatter.28
  275.6 4.9 reduce-scatter.24
  406.1 7.4 reduce-scatter.30
  423.6 7.4 reduce-scatter.26
  440.8 7.4 reduce-scatter.22
  468.7 10.3 reduce-scatter.18
  497.1 10.3 reduce-scatter.44
  515.0 10.3 reduce-scatter.40
  528.2 10.3 reduce-scatter.32
  540.7 10.3 reduce-scatter.36
  622.2 9.4 reduce-scatter.34
  650.1 9.4 reduce-scatter.38
  661.6 9.2 reduce-scatter.42
  673.6 9.2 reduce-scatter.46
Sparse Core Ops, SparseCore 1:
  278.8 57.9 all-gather.6
  339.4 60.4 all-gather.8
where the time goes:
time: 779 us; the launch traced here: 772 us
  blocking collectives  324 us (42%)
  matrix products  197 us (25%)
  waiting for transfers between devices  126 us (16%)
  other arithmetic  82.3 us (11%)
  local copies, waits for them, and re-layouts  22 us (3%)
  between operations  18.9 us (2%)
    psum x1, blocking collectives, local(): adapter_combined = adapter_combined + lax.psum(adapter_portion, 'dp')  77.1 us
    dot_general x28, matrix products, contract_trailing(): lax.dot_general(left, right, (((1,), (1,)), ((), ())), preferred_element_...  53.7 us
    all_gather x1, waiting for transfers between devices, local(): lax.all_gather(feedforward_output_weight, 'dp', axis=1, tiled=True)  52.7 us
    all_gather x1, waiting for transfers between devices, local(): lax.all_gather(feedforward_input_weight, 'dp', axis=0, tiled=True)  47.2 us
    all_gather x1, blocking collectives, local(): lax.all_gather(adapter_down_weight, 'dp', axis=1, tiled=True)  44.5 us
    all_gather x1, blocking collectives, local(): lax.all_gather(key_matrix, 'dp', axis=0, tiled=True)  41.1 us
    all_gather x1, blocking collectives, local(): lax.all_gather(attention_output_weight, 'dp', axis=1, tiled=True)  40.8 us
    all_gather x1, blocking collectives, local(): lax.all_gather(value_matrix, 'dp', axis=0, tiled=True)  39.3 us
  transfers between devices with their start and end apart: 18, of which 6 were waited for; matrix products, arithmetic and copies ran while one was open for 22% of the time, Pallas kernels for 0%

commit v1 on v0

--- a/solution.py
+++ b/solution.py
@@ -377,7 +377,7 @@
             parameters,
             kept,
         )
-        adapter_combined = adapter_combined + lax.psum(adapter_portion, "dp")
+        adapter_combined = adapter_combined + jnp.sum(lax.all_gather(adapter_portion, "dp"), axis=0)
         result_list.append(result)
         gradient_tree.append(row_gradient)
     return (jnp.stack(result_list), jnp.stack(gradient_tree), adapter_combined)

time: 779 us -> 869 us (1.12)
  blocking collectives: 324 us -> 414 us
    all_gather x0 -> x4, blocking collectives: none -> 167 us  [local(): lax.all_gather(adapter_portion, 'dp')]
    psum x1 -> x0, blocking collectives: 77.1 us -> none  [local(): adapter_combined = adapter_combined + lax.psum(adapter_portion, 'dp')]
  transfers between devices with their start and end apart: 18 -> 18, of which waited for: 6 -> 6; matrix products, arithmetic and copies ran while one was open for 22% -> 19% of each run, Pallas kernels for 0% -> 0%
where the time goes in v1:
time: 869 us; the launch traced here: 862 us
  blocking collectives  414 us (48%)
  matrix products  193 us (22%)
  waiting for transfers between devices  128 us (15%)
  other arithmetic  89.1 us (10%)
  local copies, waits for them, and re-layouts  18.5 us (2%)
  between operations  18.5 us (2%)
    all_gather x4, blocking collectives, local(): lax.all_gather(adapter_portion, 'dp')  167 us
    dot_general x28, matrix products, contract_trailing(): lax.dot_general(left, right, (((1,), (1,)), ((), ())), preferred_element_...  55.5 us
    all_gather x1, waiting for transfers between devices, local(): lax.all_gather(feedforward_output_weight, 'dp', axis=1, tiled=True)  52.7 us
    all_gather x1, waiting for transfers between devices, local(): lax.all_gather(feedforward_input_weight, 'dp', axis=0, tiled=True)  47.6 us
    all_gather x1, blocking collectives, local(): lax.all_gather(adapter_down_weight, 'dp', axis=1, tiled=True)  44.5 us
    all_gather x1, blocking collectives, local(): lax.all_gather(key_matrix, 'dp', axis=0, tiled=True)  41.1 us
    all_gather x1, blocking collectives, local(): lax.all_gather(attention_output_weight, 'dp', axis=1, tiled=True)  40.8 us
    all_gather x1, blocking collectives, local(): lax.all_gather(value_matrix, 'dp', axis=0, tiled=True)  39.3 us
  transfers between devices with their start and end apart: 18, of which 6 were waited for; matrix products, arithmetic and copies ran while one was open for 19% of the time, Pallas kernels for 0%

profile of v1, /device:TPU:0, one launch (start us, length us, event | category | flops | bytes accessed | tf_op | source)
XLA Modules:
  0.0 861.9 jit_solution(4652846751452221084)
XLA Ops:
  12.5 44.5 %all_gather.56 = bf16[2,768,8]{2,0,1:T(2,128)(2,1)S(1)} all-gather(bf16[2,48,8]{2,0,1:T(2,128)(2,1)S(1)} %copy.57), channel_id=1, replica_groups=mesh['dp'=16,'tensor'=2] {'dp'}, dimensions={1}, use_global_device_ids=true | all-gather | bytes 26112 | tf_op jit(solution)/shard_map/all_gather | solution.py:355
  57.3 39.2 %all_gather.57 = bf16[768,384]{1,0:T(8,128)(2,1)S(1)} all-gather(bf16[48,384]{1,0:T(8,128)(2,1)} %param.20), channel_id=1, replica_groups=mesh['dp'=16,'tensor'=2] {'dp'}, dimensions={0}, use_global_device_ids=true | all-gather | bytes 626688 | tf_op jit(solution)/shard_map/all_gather | solution.py:352
  96.5 41.1 %all_gather.58 = bf16[768,384]{1,0:T(8,128)(2,1)S(1)} all-gather(bf16[48,384]{1,0:T(8,128)(2,1)} %param.21), channel_id=1, replica_groups=mesh['dp'=16,'tensor'=2] {'dp'}, dimensions={0}, use_global_device_ids=true | all-gather | bytes 626688 | tf_op jit(solution)/shard_map/all_gather | solution.py:353
  137.6 39.3 %all_gather.55 = bf16[768,384]{1,0:T(8,128)(2,1)S(1)} all-gather(bf16[48,384]{1,0:T(8,128)(2,1)} %param.22), channel_id=1, replica_groups=mesh['dp'=16,'tensor'=2] {'dp'}, dimensions={0}, use_global_device_ids=true | all-gather | bytes 626688 | tf_op jit(solution)/shard_map/all_gather | solution.py:354
  176.9 40.8 %all_gather.59 = bf16[384,768]{0,1:T(8,128)(2,1)S(1)} all-gather(bf16[384,48]{0,1:T(8,128)(2,1)} %param.26), channel_id=1, replica_groups=mesh['dp'=16,'tensor'=2] {'dp'}, dimensions={1}, use_global_device_ids=true | all-gather | bytes 626688 | tf_op jit(solution)/shard_map/all_gather | solution.py:356
  233.3 3.5 all-gather
  247.7 3.0 all-gather.3
  261.6 3.4 all-gather.2
  277.4 3.7 reduce-scatter.25.cloned.1.call-done
  281.1 3.7 fusion.185
  286.8 2.8 all_gather.68
  289.6 47.6 %all-gather.7.cloned.1.call-done = bf16[768,1536]{1,0:T(8,128)(2,1)} async-done(((bf16[48,1536]{1,0:T(8,128)(2,1)}), bf16[768,1536]{1,0:T(8,128)(2,1)}) %all-gather.7.cloned.1.call-update) | async-done | bytes 2359312 | tf_op jit(solution)/shard_map/all_gather | solution.py:357
  337.2 10.4 %fusion.11 = (f32[512,1536]{1,0:T(8,128)}, f32[512,1536]{1,0:T(8,128)}) fusion(f32[1536]{0:T(1024)S(1)} %copy-done.155, bf16[512,768]{1,0:T(8,128)(2,1)S(1)} %all_gather.68, bf16[768,1536]{1,0:T(8,128)(2,1)} %all-gather.7.cloned.1.call-done), kind=kOutput, calls=%fused_computation.39 | convolution fusion | flops 1257504768 | bytes 9443328 | tf_op jit(solution)/shard_map/dot_general | solution.py:221
  347.6 52.7 %all-gather.9.cloned.1.call-done = bf16[1536,768]{0,1:T(8,128)(2,1)} async-done(((bf16[1536,48]{0,1:T(8,128)(2,1)}), bf16[1536,768]{0,1:T(8,128)(2,1)}) %all-gather.9.cloned.1.call-update) | async-done | bytes 2359312 | tf_op jit(solution)/shard_map/all_gather | solution.py:358
  400.3 6.1 fusion.35
  408.9 9.6 %fusion.10 = (f32[512,1536]{1,0:T(8,128)S(1)}, f32[512,1536]{1,0:T(8,128)S(1)}) fusion(f32[1536]{0:T(1024)S(1)} %copy-done.155, bf16[512,768]{1,0:T(8,128)(2,1)S(1)} %all_gather.66, bf16[768,1536]{1,0:T(8,128)(2,1)} %all-gather.7.cloned.1.call-done), kind=kOutput, calls=%fused_computation.38 | convolution fusion | flops 1257504768 | bytes 9443328 | tf_op jit(solution)/shard_map/dot_general | solution.py:221
  421.3 2.6 fusion.34
  423.9 2.6 all_gather.64
  426.5 9.5 %fusion.9 = (f32[512,1536]{1,0:T(8,128)S(1)}, f32[512,1536]{1,0:T(8,128)S(1)}) fusion(f32[1536]{0:T(1024)S(1)} %copy-done.155, bf16[512,768]{1,0:T(8,128)(2,1)S(1)} %all_gather.64, bf16[768,1536]{1,0:T(8,128)(2,1)} %all-gather.7.cloned.1.call-done), kind=kOutput, calls=%fused_computation.37 | convolution fusion | flops 1257504768 | bytes 9443328 | tf_op jit(solution)/shard_map/dot_general | solution.py:221
  443.0 5.9 reduce-scatter.23.cloned.1.call-done
  448.9 4.5 fusion.184
  455.7 8.1 fusion.8
  469.2 10.4 %reduce-scatter.19.cloned.1.call-done = f32[256,768]{1,0:T(8,128)} async-done(((f32[512,768]{1,0:T(8,128)}), f32[256,768]{1,0:T(8,128)}) %reduce-scatter.19.cloned.1.call-update) | async-done | bytes 786448 | tf_op jit(solution)/shard_map/reduce_scatter | solution.py:231
  481.5 2.9 fusion.79
  489.1 7.8 fusion.43
  497.0 3.8 fusion.178
  504.3 8.1 fusion.42
  513.7 2.9 all_gather.69
  516.6 8.3 fusion.40
  528.7 7.8 fusion.41
  536.6 2.8 pad_maximum_fusion.1
  539.5 3.1 multiply_reduce_fusion.7
  542.6 5.9 reduce-scatter.37.cloned.1.call-done
  548.5 2.6 fusion.176
  551.2 2.6 fusion.177
  586.7 4.7 multiply_reduce_fusion.3
  591.4 6.5 multiply_convert_fusion.3
  602.8 4.7 multiply_reduce_fusion.2
  607.5 5.0 multiply_convert_fusion.2
  615.0 8.1 multiply_reduce_fusion.1
  623.2 4.7 multiply_reduce_fusion
  628.0 45.8 %all_gather.77 = f32[16,2,8,384]{3,2,1,0:T(8,128)} all-gather(f32[1,2,8,384]{3,2,1,0:T(8,128)S(1)} %maximum_multiply_fusion), channel_id=1, replica_groups=mesh['dp'=16,'tensor'=2] {'dp'}, dimensions={0}, use_global_device_ids=true | all-gather | bytes 417792 | tf_op jit(solution)/shard_map/all_gather | solution.py:380
  677.5 40.4 %all_gather.78 = f32[16,2,8,384]{3,2,1,0:T(8,128)} all-gather(f32[1,2,8,384]{3,2,1,0:T(8,128)S(1)} %maximum_multiply_fusion.1), channel_id=1, replica_groups=mesh['dp'=16,'tensor'=2] {'dp'}, dimensions={0}, use_global_device_ids=true | all-gather | bytes 417792 | tf_op jit(solution)/shard_map/all_gather | solution.py:380
  717.8 6.7 multiply_convert_fusion.1
  726.3 4.7 multiply_convert_fusion
  747.9 42.9 %all_gather.79 = f32[16,2,8,384]{3,2,1,0:T(8,128)} all-gather(f32[1,2,8,384]{3,2,1,0:T(8,128)} %maximum_multiply_fusion.2), channel_id=1, replica_groups=mesh['dp'=16,'tensor'=2] {'dp'}, dimensions={0}, use_global_device_ids=true | all-gather | bytes 417792 | tf_op jit(solution)/shard_map/all_gather | solution.py:380
  803.8 37.8 %all_gather.160 = f32[16,2,8,384]{3,2,1,0:T(8,128)S(1)} all-gather(f32[1,2,8,384]{3,2,1,0:T(8,128)S(1)} %maximum_multiply_fusion.3), channel_id=1, replica_groups=mesh['dp'=16,'tensor'=2] {'dp'}, dimensions={0}, use_global_device_ids=true | all-gather | bytes 417792 | tf_op jit(solution)/shard_map/all_gather | solution.py:380
  851.2 3.1 pad_maximum_fusion
  (567 shorter events, 174.9 us)
Async XLA Ops:
  8.0 269.3 %reduce-scatter.21.cloned.1.call-start = ((), (), s32[]{:S(2)}) async-start(), calls=%async_computation.20 | async-start | bytes 2359296 | tf_op jit(solution)/shard_map/reduce_scatter | solution.py:212
  57.3 207.6 %copy-start.79 = (bf16[2,768,8]{1,2,0:T(8,128)(2,1)}, bf16[2,768,8]{1,2,0:T(8,128)(2,1)S(1)}, u32[]{:S(2)}) copy-start(bf16[2,768,8]{1,2,0:T(8,128)(2,1)S(1)} %copy.58) | copy-start | bytes 73732
  57.3 160.3 %copy-start.50 = (bf16[4,256,768]{2,1,0:T(8,128)(2,1)S(1)}, bf16[4,256,768]{2,1,0:T(8,128)(2,1)}, u32[]{:S(2)}) copy-start(bf16[4,256,768]{2,1,0:T(8,128)(2,1)} %param.17) | copy-start | bytes 4718596
  96.5 168.7 %copy-start.19 = (bf16[768,384]{1,0:T(8,128)(2,1)}, bf16[768,384]{1,0:T(8,128)(2,1)S(1)}, u32[]{:S(2)}) copy-start(bf16[768,384]{1,0:T(8,128)(2,1)S(1)} %all_gather.57) | copy-start | bytes 1769476
  137.6 130.3 %copy-start.14 = (bf16[768,384]{1,0:T(8,128)(2,1)}, bf16[768,384]{1,0:T(8,128)(2,1)S(1)}, u32[]{:S(2)}) copy-start(bf16[768,384]{1,0:T(8,128)(2,1)S(1)} %all_gather.58) | copy-start | bytes 1769476
  176.9 94.2 %copy-start.22 = (bf16[768,384]{1,0:T(8,128)(2,1)}, bf16[768,384]{1,0:T(8,128)(2,1)S(1)}, u32[]{:S(2)}) copy-start(bf16[768,384]{1,0:T(8,128)(2,1)S(1)} %all_gather.55) | copy-start | bytes 1769476
  217.7 56.5 %copy-start.24 = (bf16[384,768]{0,1:T(8,128)(2,1)}, bf16[384,768]{0,1:T(8,128)(2,1)S(1)}, u32[]{:S(2)}) copy-start(bf16[384,768]{0,1:T(8,128)(2,1)S(1)} %all_gather.59) | copy-start | bytes 1769476
  233.2 44.2 %reduce-scatter.17.cloned.1.call-start = ((), (), s32[]{:S(2)}) async-start(), calls=%async_computation.16 | async-start | bytes 2359296 | tf_op jit(solution)/shard_map/reduce_scatter | solution.py:212
  247.7 29.7 %reduce-scatter.29.cloned.1.call-start = ((), (), s32[]{:S(2)}) async-start(), calls=%async_computation.24 | async-start | bytes 2359296 | tf_op jit(solution)/shard_map/reduce_scatter | solution.py:212
  261.6 19.5 %reduce-scatter.25.cloned.1.call-start = ((), (), s32[]{:S(2)}) async-start(), calls=%async_computation.22 | async-start | bytes 2359296 | tf_op jit(solution)/shard_map/reduce_scatter | solution.py:212
  267.4 289.4 %copy-start.48 = (pred[512,512]{0,1:T(8,128)(4,1)}, pred[512,512]{0,1:T(8,128)(4,1)S(1)}, u32[]{:S(2)}) copy-start(pred[512,512]{0,1:T(8,128)(4,1)S(1)} %compare_and_fusion.1) | copy-start | bytes 786436
  271.0 285.8 %copy-start.125 = (f32[6,512]{1,0:T(8,128)}, f32[6,512]{1,0:T(8,128)S(1)}, u32[]{:S(2)}) copy-start(f32[6,512]{1,0:T(8,128)S(1)} %log_add_fusion.1) | copy-start | bytes 36868
  276.0 61.2 %all-gather.7.cloned.1.call-start = ((), (), s32[]{:S(2)}) async-start(), calls=%async_computation.17 | async-start | bytes 2506752 | tf_op jit(solution)/shard_map/all_gather | solution.py:357
  276.5 123.8 %all-gather.9.cloned.1.call-start = ((), (), s32[]{:S(2)}) async-start(), calls=%async_computation.18 | async-start | bytes 2506752 | tf_op jit(solution)/shard_map/all_gather | solution.py:358
  277.1 165.8 %reduce-scatter.31.cloned.1.call-start = ((), (), s32[]{:S(2)}) async-start(), calls=%async_computation.25 | async-start | bytes 2359296 | tf_op jit(solution)/shard_map/reduce_scatter | solution.py:231
  285.0 52.2 %copy-start.155 = (f32[1536]{0:T(1024)S(1)}, f32[1536]{0:T(1024)}, u32[]{:S(2)}) copy-start(f32[1536]{0:T(1024)} %param.28) | copy-start | bytes 18436
  285.5 163.4 %copy-start.139 = (f32[256]{0:T(256)}, f32[256]{0:T(256)S(1)}, u32[]{:S(2)}) copy-start(f32[256]{0:T(256)S(1)} %fusion.150) | copy-start | bytes 3076
  406.5 36.5 %reduce-scatter.27.cloned.1.call-start = ((), (), s32[]{:S(2)}) async-start(), calls=%async_computation.23 | async-start | bytes 2359296 | tf_op jit(solution)/shard_map/reduce_scatter | solution.py:231
  408.9 12.4 %copy-start.4 = (bf16[1536,768]{0,1:T(8,128)(2,1)S(1)}, bf16[1536,768]{0,1:T(8,128)(2,1)}, u32[]{:S(2)}) copy-start(bf16[1536,768]{0,1:T(8,128)(2,1)} %all-gather.9.cloned.1.call-done) | copy-start | bytes 7077892
  423.9 25.0 %reduce-scatter.23.cloned.1.call-start = ((), (), s32[]{:S(2)}) async-start(), calls=%async_computation.21 | async-start | bytes 2359296 | tf_op jit(solution)/shard_map/reduce_scatter | solution.py:231
  441.3 38.3 %reduce-scatter.19.cloned.1.call-start = ((), (), s32[]{:S(2)}) async-start(), calls=%async_computation.19 | async-start | bytes 2359296 | tf_op jit(solution)/shard_map/reduce_scatter | solution.py:231
  469.2 70.3 %reduce-scatter.45.cloned.1.call-start = ((), (), s32[]{:S(2)}) async-start(), calls=%async_computation.32 | async-start | bytes 2359296 | tf_op jit(solution)/shard_map/reduce_scatter | solution.py:273
  485.6 53.9 %copy-start.137 = (f32[256]{0:T(256)}, f32[256]{0:T(256)S(1)}, u32[]{:S(2)}) copy-start(f32[256]{0:T(256)S(1)} %negate_multiply_fusion.5) | copy-start | bytes 3076
  496.9 42.6 %reduce-scatter.41.cloned.1.call-start = ((), (), s32[]{:S(2)}) async-start(), calls=%async_computation.30 | async-start | bytes 2359296 | tf_op jit(solution)/shard_map/reduce_scatter | solution.py:273
  512.4 27.1 %reduce-scatter.33.cloned.1.call-start = ((), (), s32[]{:S(2)}) async-start(), calls=%async_computation.26 | async-start | bytes 2359296 | tf_op jit(solution)/shard_map/reduce_scatter | solution.py:273
  524.9 23.6 %reduce-scatter.37.cloned.1.call-start = ((), (), s32[]{:S(2)}) async-start(), calls=%async_computation.28 | async-start | bytes 2359296 | tf_op jit(solution)/shard_map/reduce_scatter | solution.py:273
  536.6 307.1 %reduce-scatter.35.cloned.1.call-start = ((), (), s32[]{:S(2)}) async-start(), calls=%async_computation.27 | async-start | bytes 1179648 | tf_op jit(solution)/shard_map/reduce_scatter | solution.py:301
  551.1 15.6 %copy-start.33 = (f32[256,768]{1,0:T(8,128)}, f32[256,768]{1,0:T(8,128)S(1)}, u32[]{:S(2)}) copy-start(f32[256,768]{1,0:T(8,128)S(1)} %get-tuple-element.191) | copy-start | bytes 2359300
  569.7 12.6 %slice-start.2 = ((s8[6291456]{0:T(1024)(128)(4,1)}), s8[4194304]{0:T(1024)(128)(4,1)S(1)}, s32[]{:S(2)}) async-start(s8[6291456]{0:T(1024)(128)(4,1)} %bitcast.412), calls=%async_computation.36 | async-start | bytes 8388608
  623.2 50.6 %copy-start.15 = (bf16[768,384]{1,0:T(8,128)(2,1)S(1)}, bf16[768,384]{1,0:T(8,128)(2,1)}, u32[]{:S(2)}) copy-start(bf16[768,384]{1,0:T(8,128)(2,1)} %copy-done.14) | copy-start | bytes 1769476
  623.2 50.6 %copy-start.93 = (bf16[6,64,512]{2,1,0:T(8,128)(2,1)S(1)}, bf16[6,64,512]{2,1,0:T(8,128)(2,1)}, u32[]{:S(2)}) copy-start(bf16[6,64,512]{2,1,0:T(8,128)(2,1)} %fusion.53) | copy-start | bytes 1179652
  623.2 51.2 %copy-start.80 = (bf16[2,768,8]{1,2,0:T(8,128)(2,1)S(1)}, bf16[2,768,8]{1,2,0:T(8,128)(2,1)}, u32[]{:S(2)}) copy-start(bf16[2,768,8]{1,2,0:T(8,128)(2,1)} %copy-done.79) | copy-start | bytes 73732
  627.9 47.3 %copy-start.55 = (f32[512,768]{1,0:T(8,128)S(1)}, f32[512,768]{1,0:T(8,128)}, u32[]{:S(2)}) copy-start(f32[512,768]{1,0:T(8,128)} %fusion.213) | copy-start | bytes 4718596
  627.9 47.4 %copy-start.56 = (f32[512,768]{1,0:T(8,128)S(1)}, f32[512,768]{1,0:T(8,128)}, u32[]{:S(2)}) copy-start(f32[512,768]{1,0:T(8,128)} %fusion.211) | copy-start | bytes 4718596
  627.9 47.4 %copy-start.130 = (f32[512,8]{0,1:T(8,128)S(1)}, f32[512,8]{0,1:T(8,128)}, u32[]{:S(2)}) copy-start(f32[512,8]{0,1:T(8,128)} %convolution_multiply_fusion.22) | copy-start | bytes 49156
  675.3 42.5 %copy-start.134 = (f32[6,512]{1,0:T(8,128)S(1)}, f32[6,512]{1,0:T(8,128)}, u32[]{:S(2)}) copy-start(f32[6,512]{1,0:T(8,128)} %get-tuple-element.345) | copy-start | bytes 36868
  677.4 168.4 %reduce-scatter.39.cloned.1.call-start = ((), (), s32[]{:S(2)}) async-start(), calls=%async_computation.29 | async-start | bytes 1179648 | tf_op jit(solution)/shard_map/reduce_scatter | solution.py:301
  717.8 8.4 slice-start.4
  738.9 109.0 %reduce-scatter.43.cloned.1.call-start = ((), (), s32[]{:S(2)}) async-start(), calls=%async_computation.31 | async-start | bytes 1179648 | tf_op jit(solution)/shard_map/reduce_scatter | solution.py:301
  745.7 50.0 %copy-start.131 = (f32[512,8]{0,1:T(8,128)S(1)}, f32[512,8]{0,1:T(8,128)}, u32[]{:S(2)}) copy-start(f32[512,8]{0,1:T(8,128)} %convolution_multiply_fusion.17) | copy-start | bytes 49156
  747.8 51.2 %copy-start.11 = (bf16[6,512,512]{1,2,0:T(8,128)(2,1)S(1)}, bf16[6,512,512]{1,2,0:T(8,128)(2,1)}, u32[]{:S(2)}) copy-start(bf16[6,512,512]{1,2,0:T(8,128)(2,1)} %copy-done.10) | copy-start | bytes 9437188
  747.8 102.2 %reduce-scatter.47.cloned.1.call-start = ((), (), s32[]{:S(2)}) async-start(), calls=%async_computation.33 | async-start | bytes 1179648 | tf_op jit(solution)/shard_map/reduce_scatter | solution.py:301
  800.8 42.9 %copy-start.34 = (f32[256,768]{1,0:T(8,128)S(1)}, f32[256,768]{1,0:T(8,128)}, u32[]{:S(2)}) copy-start(f32[256,768]{1,0:T(8,128)} %copy-done.33) | copy-start | bytes 2359300
  800.8 42.8 %copy-start.146 = (f32[256]{0:T(256)S(1)}, f32[256]{0:T(256)}, u32[]{:S(2)}) copy-start(f32[256]{0:T(256)} %copy-done.145) | copy-start | bytes 3076
  802.9 42.8 %copy-start.36 = (f32[256,768]{1,0:T(8,128)S(1)}, f32[256,768]{1,0:T(8,128)}, u32[]{:S(2)}) copy-start(f32[256,768]{1,0:T(8,128)} %copy-done.35) | copy-start | bytes 2359300
  802.9 42.8 %copy-start.144 = (f32[256]{0:T(256)S(1)}, f32[256]{0:T(256)}, u32[]{:S(2)}) copy-start(f32[256]{0:T(256)} %copy-done.143) | copy-start | bytes 3076
  802.9 44.9 %copy-start.32 = (f32[256,768]{1,0:T(8,128)S(1)}, f32[256,768]{1,0:T(8,128)}, u32[]{:S(2)}) copy-start(f32[256,768]{1,0:T(8,128)} %copy-done.31) | copy-start | bytes 2359300
  802.9 44.9 %copy-start.142 = (f32[256]{0:T(256)S(1)}, f32[256]{0:T(256)}, u32[]{:S(2)}) copy-start(f32[256]{0:T(256)} %copy-done.141) | copy-start | bytes 3076
  (136 other events, 487.8 us)
Sparse Core Ops, SparseCore 0:
  233.3 4.9 reduce-scatter.20
  247.8 5.0 reduce-scatter.16
  261.7 5.0 reduce-scatter.28
  276.1 4.9 reduce-scatter.24
  406.6 7.4 reduce-scatter.30
  424.0 7.4 reduce-scatter.26
  441.4 7.4 reduce-scatter.22
  469.3 10.3 reduce-scatter.18
  497.0 10.3 reduce-scatter.44
  512.5 10.3 reduce-scatter.40
  525.7 10.3 reduce-scatter.32
  538.2 10.3 reduce-scatter.36
  677.5 4.0 reduce-scatter.34
  739.0 5.9 reduce-scatter.38
  748.0 8.3 reduce-scatter.42
  803.1 4.0 reduce-scatter.46
Sparse Core Ops, SparseCore 1:
  279.3 57.9 all-gather.6
  339.9 60.4 all-gather.8
